TPU v7x, 32 devices: a whole 2x2x4 slice. The times are simulated.
32 devices in a mesh: gx: 4 (over z), gy: 4 (over x, core), gz: 2 (over y).
Axes of the slice: x: 2, y: 2, z: 4, core: 2. Of those that a mesh axis runs over, the one named last changes fastest.
Arguments:
- pair: bfloat16 [1024, 1024, 128], P('gx', 'gy'), may hold values from -8 to 8, as said below
- residue_mask: int32 [1024], replicated, may hold values 0 or 1
- ln_in_gain: float32 [128], replicated, may hold values from 0.1 to 1.9
- w_proj: bfloat16 [128, 4, 128], P(None, None, 'gz'), may hold values from -0.5 to 0.5
- w_gate: bfloat16 [128, 128], replicated, may hold values from -0.5 to 0.5
- ln_out_gain: float32 [128], replicated, may hold values from 0.1 to 1.9
- w_out: bfloat16 [128, 128], replicated, may hold values from -0.5 to 0.5
Outputs:
- update: bfloat16 [128, 1024, 1024], P(None, ('gx', 'gz'), 'gy')
- energy: float32 [], replicated
Inputs may be any that keep to these rules, and one draw needn't show every extreme that they name: pair is symmetric in its two residue indices: pair[i, j, c] equals pair[j, i, c].
All inputs are finite; a program needn't handle non-finite values.
Results may differ from a plain program's by a relative error of at most 0.0083.
Values may be sent and summed in bfloat16 or wider, within the bound.
A program may use at most 256 MiB of HBM per device.

v0:
```python
import jax
import jax.numpy as jnp
from jax import lax
from jax.sharding import PartitionSpec as P

NORM_EPS = 1e-05


def layer_norm(values, gain_vec, axis):
    mean_val = jnp.mean(values, axis=axis, keepdims=True)
    centred = values - mean_val
    variance = jnp.mean(centred * centred, axis=axis, keepdims=True)
    return centred * lax.rsqrt(variance + NORM_EPS) * gain_vec


def batched(first, second):
    return jnp.einsum("hik,hkj->hij", first, second, preferred_element_type=jnp.float32)


def local(pair, residue_mask, ln_in_gain, w_proj, w_gate, ln_out_gain, w_out):
    tile_len = pair.shape[0]
    channel_count = pair.shape[2]
    grid_len = lax.axis_size("gx")
    slab_count = lax.axis_size("gz")
    slab_rows = tile_len // slab_count
    total_len = tile_len * grid_len
    row_block = lax.axis_index("gx")
    col_block = lax.axis_index("gy")
    slab_index = lax.axis_index("gz")
    mask_float = residue_mask.astype(jnp.float32)
    row_mask = lax.dynamic_slice_in_dim(mask_float, row_block * tile_len, tile_len)
    col_mask = lax.dynamic_slice_in_dim(mask_float, col_block * tile_len, tile_len)
    tile_mask = row_mask[:, None] * col_mask[None, :]
    normed = layer_norm(pair.astype(jnp.float32), ln_in_gain, -1).astype(jnp.bfloat16)
    projected = jnp.einsum("ijd,dkh->khij", normed, w_proj, preferred_element_type=jnp.float32)
    left_tile = (tile_mask * jax.nn.sigmoid(projected[0]) * projected[1]).astype(jnp.bfloat16)
    right_tile = (tile_mask * jax.nn.sigmoid(projected[2]) * projected[3]).astype(jnp.bfloat16)
    col_left, col_right = (
        lax.all_gather(left_tile, "gx", axis=1, tiled=True),
        lax.all_gather(right_tile, "gx", axis=1, tiled=True),
    )
    piece_left = lax.all_gather(left_tile, "gy", axis=2, tiled=True)
    piece_right = lax.all_gather(right_tile, "gy", axis=2, tiled=True)
    below_left = col_left
    below_right = col_right
    below_left, below_right = (below_left, below_right)
    summed = batched(piece_left, below_right) + batched(piece_right, below_left)
    tri_map = (0.5 * summed).astype(jnp.bfloat16)
    tri_normed = layer_norm(
        lax.all_to_all(tri_map, "gz", split_axis=1, concat_axis=0, tiled=True).astype(jnp.float32),
        ln_out_gain[:, None, None],
        0,
    ).astype(jnp.bfloat16)
    mixed = jnp.einsum("hij,hc->cij", tri_normed, w_out, preferred_element_type=jnp.float32)
    slab_normed = lax.dynamic_slice_in_dim(normed, slab_index * slab_rows, slab_rows, 0)
    gate_vals = jax.nn.sigmoid(
        jnp.einsum("ijd,dc->cij", slab_normed, w_gate, preferred_element_type=jnp.float32)
    )
    update = (gate_vals * mixed).astype(jnp.bfloat16)
    row_start = row_block * tile_len + slab_index * slab_rows
    row_float = (row_start + jnp.arange(slab_rows, dtype=jnp.int32)).astype(jnp.float32)
    col_float = (col_block * tile_len + jnp.arange(tile_len, dtype=jnp.int32)).astype(jnp.float32)
    slab_mask = lax.dynamic_slice_in_dim(mask_float, row_start, slab_rows)
    weighting = (
        (1.0 + (row_float[:, None] + col_float[None, :]) / total_len)
        * slab_mask[:, None]
        * col_mask[None, :]
    )
    update_float = update.astype(jnp.float32)
    partial_sum = jnp.sum(update_float * update_float * weighting[None])
    energy = lax.psum(partial_sum, ("gx", "gy", "gz")) / (total_len * total_len * channel_count)
    return (update, energy)


def solution(mesh):
    in_specs = (P("gx", "gy", None), P(), P(), P(None, None, "gz"), P(), P(), P())
    out_specs = (P(None, ("gx", "gz"), "gy"), P())
    return jax.shard_map(local, mesh=mesh, in_specs=in_specs, out_specs=out_specs, check_vma=False)
```

profile of v0, /device:TPU:12, one launch (start us, length us, event | category | flops | bytes accessed | tf_op | source)
XLA Modules:
  0.0 1946.3 jit_solution(17689445060744639698)
XLA Ops:
  7.2 0.0 copy-start
  7.2 0.0 all-gather.11.cloned.1.call-start
  7.2 0.0 copy-start.2
  7.2 0.8 convert_element_type.61
  8.1 11.7 convert_reduce_fusion
  19.8 0.0 copy-done.2
  19.8 19.0 fusion.2
  38.9 0.1 fusion.47
  39.0 0.6 copy-done.4
  39.6 0.1 broadcast_multiply_fusion
  39.7 21.9 %fusion.4 = bf16[256,256,128]{2,1,0:T(8,128)(2,1)} fusion(bf16[256,256,128]{2,1,0:T(8,128)(2,1)} %param.7, f32[128]{0:T(128)S(1)} %copy-done.7, f32[256,256]{1,0:T(8,128)S(1)} %add_rsqrt_fusion, f32[256,256]{1,0:T(8,128)S(1)} %broadcast_multiply_fusion.1), kind=kLoop, calls=%fused_computation.6 | loop fusion | flops 41943040 | bytes 34079232 | tf_op jit(solution)/shard_map/convert_element_type | solution.py:34
  61.6 35.2 %convolution_bitcast_fusion = f32[4,64,256,256]{3,1,0,2:T(8,128)} fusion(bf16[256,256,128]{2,1,0:T(8,128)(2,1)} %fusion.4, bf16[128,4,64]{0,2,1:T(8,128)(2,1)S(1)} %copy-done), kind=kOutput, calls=%fused_computation.13 | convolution fusion | flops 4294967296 | bytes 83951616 | tf_op jit(solution)/shard_map/ijd,dkh->khij/dot_general | solution.py:35
  96.8 29.8 %fusion.12 = (bf16[64,256,256]{2,0,1:T(8,128)(2,1)}, bf16[64,256,256]{2,0,1:T(8,128)(2,1)}) fusion(f32[4,64,256,256]{3,1,0,2:T(8,128)} %convolution_bitcast_fusion, f32[256,256]{1,0:T(8,128)S(1)} %broadcast_multiply_fusion), kind=kLoop, calls=%fused_computation.16 | loop fusion | flops 50331648 | bytes 84148224 | tf_op jit(solution)/shard_map/convert_element_type | solution.py:37
  126.6 0.0 all-gather.11.cloned.1.call-update
  126.7 0.0 all-gather.9.cloned.1.call-start
  126.7 0.7 all-gather.9.cloned.1.call-update
  127.4 0.0 all-gather.5.cloned.1.call-start
  127.5 0.7 all-gather.5.cloned.1.call-update
  128.2 0.2 all-gather.7.cloned.1.call-start
  128.4 0.3 all-gather.7.cloned.1.call-update
  128.7 557.8 %all-gather.11.cloned.1.call-done = bf16[64,1024,256]{2,0,1:T(8,128)(2,1)} async-done(((bf16[64,256,256]{2,0,1:T(8,128)(2,1)}), bf16[64,1024,256]{2,0,1:T(8,128)(2,1)}) %all-gather.11.cloned.1.call-update) | async-done | bytes 33554448 | tf_op jit(solution)/shard_map/all_gather | solution.py:39
  686.6 209.1 %all-gather.9.cloned.1.call-done = bf16[64,256,1024]{2,0,1:T(8,128)(2,1)} async-done(((bf16[64,256,256]{2,0,1:T(8,128)(2,1)}), bf16[64,256,1024]{2,0,1:T(8,128)(2,1)}) %all-gather.9.cloned.1.call-update) | async-done | bytes 33554448 | tf_op jit(solution)/shard_map/all_gather | solution.py:43
  895.7 51.4 %fusion.5 = f32[64,256,256]{2,1,0:T(8,128)} fusion(bf16[64,1024,256]{2,0,1:T(8,128)(2,1)} %all-gather.11.cloned.1.call-done, bf16[64,256,1024]{2,0,1:T(8,128)(2,1)} %all-gather.9.cloned.1.call-done), kind=kOutput, calls=%fused_computation.7 | convolution fusion | flops 8589934592 | bytes 83886080 | tf_op jit(solution)/shard_map/hik,hkj->hij/dot_general | solution.py:17
  947.0 156.2 %all-gather.5.cloned.1.call-done = bf16[64,256,1024]{2,0,1:T(8,128)(2,1)} async-done(((bf16[64,256,256]{2,0,1:T(8,128)(2,1)}), bf16[64,256,1024]{2,0,1:T(8,128)(2,1)}) %all-gather.5.cloned.1.call-update) | async-done | bytes 33554448 | tf_op jit(solution)/shard_map/all_gather | solution.py:42
  1103.3 560.7 %all-gather.7.cloned.1.call-done = bf16[64,1024,256]{2,0,1:T(8,128)(2,1)} async-done(((bf16[64,256,256]{2,0,1:T(8,128)(2,1)}), bf16[64,1024,256]{2,0,1:T(8,128)(2,1)}) %all-gather.7.cloned.1.call-update) | async-done | bytes 33554448 | tf_op jit(solution)/shard_map/all_gather | solution.py:40
  1663.9 64.8 %multiply_convert_fusion.1 = bf16[64,256,256]{2,1,0:T(8,128)(2,1)} fusion(f32[64,256,256]{2,1,0:T(8,128)} %fusion.5, bf16[64,1024,256]{2,0,1:T(8,128)(2,1)} %all-gather.7.cloned.1.call-done, bf16[64,256,1024]{2,0,1:T(8,128)(2,1)} %all-gather.5.cloned.1.call-done), kind=kOutput, calls=%fused_computation.43 | convolution fusion | flops 8602517504 | bytes 92274688 | tf_op jit(solution)/shard_map/hik,hkj->hij/dot_general | solution.py:17
  1728.7 0.0 copy-start.3
  1728.7 11.4 copy.45
  1740.1 7.4 all-to-all-start
  1747.5 0.7 dynamic_slice.15
  1748.3 0.1 multiply_multiply_fusion
  1748.4 11.5 fusion.37
  1759.9 78.6 %all-to-all-done = bf16[64,256,256]{2,0,1:T(8,128)(2,1)} async-done(((bf16[64,256,256]{2,0,1:T(8,128)(2,1)}), bf16[64,256,256]{2,0,1:T(8,128)(2,1)}, u32[]{:S(2)}, u32[]{:S(2)}) %all-to-all-start) | async-done | bytes 8388640 | tf_op jit(solution)/shard_map/all_to_all | solution.py:50
  1838.5 11.5 fusion.46
  1850.0 1.2 fusion.35
  1851.2 2.2 multiply_reduce_fusion.1
  1853.4 0.0 copy-start.8
  1853.4 0.0 slice-start
  1853.5 0.0 slice-start.1
  1853.5 0.0 slice-start.2
  1853.5 7.7 copy.47
  1861.2 0.0 slice-start.3
  1861.2 0.0 copy-start.9
  1861.2 5.6 fusion.30
  1866.9 0.0 copy-start.1
  1866.9 14.6 multiply_reduce_fusion
  1881.4 12.7 copy.49
  1894.2 43.7 %psum.7 = f32[]{:T(128)} all-reduce(f32[]{:T(128)} %get-tuple-element.16), channel_id=1, replica_groups=mesh['gx'=4,'gy'=4,'gz'=2] {'gx','gy','gz'}, use_global_device_ids=true, to_apply=%region_5.0 | all-reduce | flops 1 | bytes 8 | tf_op jit(solution)/shard_map/psum | solution.py:71
  (23 shorter events, 0.1 us)
Async XLA Ops:
  7.2 54.5 %copy-start = (bf16[128,4,64]{0,2,1:T(8,128)(2,1)S(1)}, bf16[128,4,64]{0,2,1:T(8,128)(2,1)}, u32[]{:S(2)}) copy-start(bf16[128,4,64]{0,2,1:T(8,128)(2,1)} %param.10) | copy-start | bytes 196612
  7.2 679.4 %all-gather.11.cloned.1.call-start = ((), (), s32[]{:S(2)}) async-start(), calls=%async_computation.4 | async-start | bytes 41943040 | tf_op jit(solution)/shard_map/all_gather | solution.py:39
  7.2 12.6 copy-start.2
  8.1 30.8 %copy-start.6 = (f32[1024]{0:T(1024)}, f32[1024]{0:T(1024)S(1)}, u32[]{:S(2)}) copy-start(f32[1024]{0:T(1024)S(1)} %convert_element_type.61) | copy-start | bytes 12292
  8.1 31.6 %copy-start.7 = (f32[128]{0:T(128)S(1)}, f32[128]{0:T(128)}, u32[]{:S(2)}) copy-start(f32[128]{0:T(128)} %param.9) | copy-start | bytes 1540
  39.0 0.6 copy-start.4
  126.7 769.0 %all-gather.9.cloned.1.call-start = ((), (), s32[]{:S(2)}) async-start(), calls=%async_computation.3 | async-start | bytes 41943040 | tf_op jit(solution)/shard_map/all_gather | solution.py:43
  127.4 975.8 %all-gather.5.cloned.1.call-start = ((), (), s32[]{:S(2)}) async-start(), calls=%async_computation.1 | async-start | bytes 41943040 | tf_op jit(solution)/shard_map/all_gather | solution.py:42
  128.2 1535.8 %all-gather.7.cloned.1.call-start = ((), (), s32[]{:S(2)}) async-start(), calls=%async_computation.2 | async-start | bytes 41943040 | tf_op jit(solution)/shard_map/all_gather | solution.py:40
  1728.7 19.6 %copy-start.5 = (f32[256]{0:T(256)S(1)}, f32[256]{0:T(256)}, u32[]{:S(2)}) copy-start(f32[256]{0:T(256)} %copy-done.4) | copy-start | bytes 3076
  1728.7 19.7 %copy-start.3 = (bf16[128,128]{1,0:T(8,128)(2,1)S(1)}, bf16[128,128]{1,0:T(8,128)(2,1)}, u32[]{:S(2)}) copy-start(bf16[128,128]{1,0:T(8,128)(2,1)} %param.11) | copy-start | bytes 98308
  1740.1 98.3 %all-to-all-start = ((bf16[64,256,256]{2,0,1:T(8,128)(2,1)}), bf16[64,256,256]{2,0,1:T(8,128)(2,1)}, u32[]{:S(2)}, u32[]{:S(2)}) async-start(bf16[64,256,256]{2,0,1:T(8,128)(2,1)} %copy.45), calls=%async_computation | async-start | bytes 16777216 | tf_op jit(solution)/shard_map/all_to_all | solution.py:50
  1853.4 7.8 copy-start.8
  1853.4 13.4 slice-start
  1853.5 13.4 slice-start.1
  1853.5 13.4 slice-start.2
  1861.2 5.6 slice-start.3
  1861.2 5.6 copy-start.9
  1866.9 71.6 %copy-start.1 = (bf16[128,4,64]{0,2,1:T(8,128)(2,1)S(1)}, bf16[128,4,64]{0,2,1:T(8,128)(2,1)}, u32[]{:S(2)}) copy-start(bf16[128,4,64]{0,2,1:T(8,128)(2,1)} %param.10) | copy-start | bytes 196612
Sparse Core Ops, SparseCore 0:
  126.8 559.7 all-gather.10
  688.7 206.9 all-gather.8
  897.2 205.9 all-gather.4
  1105.2 558.6 all-gather.6
where the time goes:
time: 1950 us
  waiting for transfers between devices  1560 us (80%)
  matrix products  177 us (9%)
  other arithmetic  104 us (5%)
  blocking collectives  43.7 us (2%)
  local copies, waits for them, and re-layouts  33.3 us (2%)
    all_gather x1, waiting for transfers between devices, local(): lax.all_gather(right_tile, 'gx', axis=1, tiled=True)  561 us
    all_gather x1, waiting for transfers between devices, local(): lax.all_gather(left_tile, 'gx', axis=1, tiled=True)  558 us
    all_gather x1, waiting for transfers between devices, local(): piece_right = lax.all_gather(right_tile, 'gy', axis=2, tiled=True)  209 us
    all_gather x1, waiting for transfers between devices, local(): piece_left = lax.all_gather(left_tile, 'gy', axis=2, tiled=True)  156 us
    dot_general x2, matrix products, batched(): jnp.einsum('hik,hkj->hij', first, second, preferred_element_type=jnp.floa...  116 us
    all_to_all x1, waiting for transfers between devices, local(): lax.all_to_all(tri_map, 'gz', split_axis=1, concat_axis=0, tiled=True)  78.6 us
    psum x1, blocking collectives, local(): lax.psum(partial_sum, ('gx', 'gy', 'gz'))  43.7 us
  transfers between devices with their start and end apart: 5, of which 5 were waited for; matrix products, arithmetic and copies ran while one was open for 3% of the time, Pallas kernels for 0%

commit v1 on v0

--- a/solution.py
+++ b/solution.py
@@ -4,6 +4,17 @@
 from jax.sharding import PartitionSpec as P
 
 NORM_EPS = 1e-05
+
+
+def turned_line(value, name, dim):
+    size = lax.axis_size(name)
+    right = [(i, (i + 1) % size) for i in range(size)]
+    shards = [value]
+    for far in range(1, size):
+        shards = [lax.ppermute(shards[0], name, right), *shards]
+    result = jnp.concatenate(shards, axis=dim)
+    shift = (lax.axis_index(name) + 1) * shards[-1].shape[dim]
+    return jnp.roll(result, shift, axis=dim)
 
 
 def layer_norm(values, gain_vec, axis):
@@ -39,7 +50,7 @@
         lax.all_gather(left_tile, "gx", axis=1, tiled=True),
         lax.all_gather(right_tile, "gx", axis=1, tiled=True),
     )
-    piece_left = lax.all_gather(left_tile, "gy", axis=2, tiled=True)
+    piece_left = turned_line(left_tile, "gy", 2)
     piece_right = lax.all_gather(right_tile, "gy", axis=2, tiled=True)
     below_left = col_left
     below_right = col_right

time: 1950 us -> 1750 us (0.90)
  waiting for transfers between devices: 1560 us -> 1260 us
  local copies, waits for them, and re-layouts: 33.3 us -> 128 us
    all_gather x1, waiting for transfers between devices: 558 us -> 185 us  [local(): lax.all_gather(left_tile, 'gx', axis=1, tiled=True)]
    ppermute x0 -> x3, waiting for transfers between devices: none -> 279 us  [turned_line(): shards = [lax.ppermute(shards[0], name, right), *shards]]
    all_gather x1 -> x0, waiting for transfers between devices: 156 us -> none  [local(): piece_left = lax.all_gather(left_tile, 'gy', axis=2, tiled=True)]
    unnamed x29 -> x38, local copies, waits for them, and re-layouts: 13.4 us -> 76 us
    all_gather x1, waiting for transfers between devices: 561 us -> 509 us  [local(): lax.all_gather(right_tile, 'gx', axis=1, tiled=True)]
    dynamic_slice x0 -> x1, local copies, waits for them, and re-layouts: none -> 23.3 us  [turned_line(): return jnp.roll(result, shift, axis=dim)]
  transfers between devices with their start and end apart: 5 -> 7, of which waited for: 5 -> 7; matrix products, arithmetic and copies ran while one was open for 3% -> 9% of each run, Pallas kernels for 0% -> 0%
where the time goes in v1:
time: 1750 us; the launch traced here: 1740 us
  waiting for transfers between devices  1260 us (72%)
  matrix products  178 us (10%)
  local copies, waits for them, and re-layouts  128 us (7%)
  other arithmetic  104 us (6%)
  blocking collectives  43.7 us (2%)
    all_gather x1, waiting for transfers between devices, local(): lax.all_gather(right_tile, 'gx', axis=1, tiled=True)  509 us
    ppermute x3, waiting for transfers between devices, turned_line(): shards = [lax.ppermute(shards[0], name, right), *shards]  279 us
    all_gather x1, waiting for transfers between devices, local(): piece_right = lax.all_gather(right_tile, 'gy', axis=2, tiled=True)  209 us
    all_gather x1, waiting for transfers between devices, local(): lax.all_gather(left_tile, 'gx', axis=1, tiled=True)  185 us
    dot_general x2, matrix products, batched(): jnp.einsum('hik,hkj->hij', first, second, preferred_element_type=jnp.floa...  116 us
    all_to_all x1, waiting for transfers between devices, local(): lax.all_to_all(tri_map, 'gz', split_axis=1, concat_axis=0, tiled=True)  78.6 us
    unnamed x38, local copies, waits for them, and re-layouts  76 us
    psum x1, blocking collectives, local(): lax.psum(partial_sum, ('gx', 'gy', 'gz'))  43.7 us
  transfers between devices with their start and end apart: 7, of which 7 were waited for; matrix products, arithmetic and copies ran while one was open for 9% of the time, Pallas kernels for 0%

profile of v1, /device:TPU:12, one launch (start us, length us, event | category | flops | bytes accessed | tf_op | source)
XLA Modules:
  0.0 1738.8 jit_solution(7913512375947977390)
XLA Ops:
  7.2 0.0 all-gather.8.cloned.1.call-start
  7.2 0.8 convert_element_type.61
  8.1 11.7 convert_reduce_fusion
  19.8 19.0 %fusion.2 = f32[256,256]{1,0:T(8,128)S(1)} fusion(bf16[256,256,128]{2,1,0:T(8,128)(2,1)S(1)} %copy-done.2, f32[256,256]{1,0:T(8,128)S(1)} %broadcast_multiply_fusion.1), kind=kLoop, calls=%fused_computation.4 | loop fusion | flops 33488896 | bytes 17301504 | tf_op jit(solution)/shard_map/reduce_sum | solution.py:23
  38.9 0.1 fusion.47
  39.0 0.6 copy-done.5
  39.6 0.1 broadcast_multiply_fusion
  39.7 21.9 %fusion.4 = bf16[256,256,128]{2,1,0:T(8,128)(2,1)} fusion(bf16[256,256,128]{2,1,0:T(8,128)(2,1)} %param.7, f32[128]{0:T(128)S(1)} %copy-done.8, f32[256,256]{1,0:T(8,128)S(1)} %add_rsqrt_fusion, f32[256,256]{1,0:T(8,128)S(1)} %broadcast_multiply_fusion.1), kind=kLoop, calls=%fused_computation.6 | loop fusion | flops 41943040 | bytes 34079232 | tf_op jit(solution)/shard_map/convert_element_type | solution.py:45
  61.6 35.3 %convolution_bitcast_fusion = f32[4,64,256,256]{3,1,0,2:T(8,128)} fusion(bf16[256,256,128]{2,1,0:T(8,128)(2,1)} %fusion.4, bf16[128,4,64]{0,2,1:T(8,128)(2,1)S(1)} %copy-done), kind=kOutput, calls=%fused_computation.13 | convolution fusion | flops 4294967296 | bytes 83951616 | tf_op jit(solution)/shard_map/ijd,dkh->khij/dot_general | solution.py:46
  96.9 29.8 %fusion.12 = (bf16[64,256,256]{2,0,1:T(8,128)(2,1)}, bf16[64,256,256]{2,0,1:T(8,128)(2,1)}) fusion(f32[4,64,256,256]{3,1,0,2:T(8,128)} %convolution_bitcast_fusion, f32[256,256]{1,0:T(8,128)S(1)} %broadcast_multiply_fusion), kind=kLoop, calls=%fused_computation.16 | loop fusion | flops 50331648 | bytes 84148224 | tf_op jit(solution)/shard_map/convert_element_type | solution.py:48
  126.7 0.0 all-gather.6.cloned.1.call-start
  126.8 0.7 all-gather.6.cloned.1.call-update
  127.5 0.0 all-gather.4.cloned.1.call-start
  127.5 0.7 all-gather.4.cloned.1.call-update
  128.2 0.1 collective-permute-start
  128.3 93.1 %collective-permute-done = bf16[64,256,256]{2,0,1:T(8,128)(2,1)S(1)} collective-permute-done((bf16[64,256,256]{2,0,1:T(8,128)(2,1)}, bf16[64,256,256]{2,0,1:T(8,128)(2,1)S(1)}, u32[]{:S(2)}, u32[]{:S(2)}) %collective-permute-start) | collective-permute-done | bytes 8388640 | tf_op jit(solution)/shard_map/ppermute | solution.py:14
  221.3 3.2 copy-done.3
  224.6 93.0 %collective-permute-done.1 = bf16[64,256,256]{2,0,1:T(8,128)(2,1)} collective-permute-done((bf16[64,256,256]{2,0,1:T(8,128)(2,1)S(1)}, bf16[64,256,256]{2,0,1:T(8,128)(2,1)}, u32[]{:S(2)}, u32[]{:S(2)}) %collective-permute-start.1) | collective-permute-done | bytes 8388640 | tf_op jit(solution)/shard_map/ppermute | solution.py:14
  317.5 0.2 collective-permute-start.2
  317.7 93.2 %collective-permute-done.2 = bf16[64,256,256]{2,0,1:T(8,128)(2,1)} collective-permute-done((bf16[64,256,256]{2,0,1:T(8,128)(2,1)}, bf16[64,256,256]{2,0,1:T(8,128)(2,1)}, u32[]{:S(2)}, u32[]{:S(2)}) %collective-permute-start.2) | collective-permute-done | bytes 8388640 | tf_op jit(solution)/shard_map/ppermute | solution.py:14
  410.9 8.4 constant_dynamic-update-slice_fusion.7
  419.3 8.6 constant_dynamic-update-slice_fusion.6
  427.9 8.5 constant_dynamic-update-slice_fusion.5
  436.4 8.4 constant_dynamic-update-slice_fusion.4
  444.8 8.5 constant_dynamic-update-slice_fusion.3
  453.3 8.4 constant_dynamic-update-slice_fusion.2
  461.7 8.6 constant_dynamic-update-slice_fusion.1
  470.3 8.5 constant_dynamic-update-slice_fusion
  478.7 23.3 %constant_dynamic-slice_fusion = bf16[64,256,1024]{2,0,1:T(8,128)(2,1)} fusion(bf16[64,256,2048]{2,0,1:T(8,128)(2,1)} %constant_dynamic-update-slice_fusion, s32[]{:T(128)S(6)} %select_n.29), kind=kLoop, calls=%fused_computation.68 | loop fusion | bytes 67108864 | tf_op jit(solution)/shard_map/jit(_roll_dynamic)/dynamic_slice | solution.py:17
  502.1 184.5 %all-gather.8.cloned.1.call-done = bf16[64,1024,256]{2,0,1:T(8,128)(2,1)} async-done(((bf16[64,256,256]{2,0,1:T(8,128)(2,1)}), bf16[64,1024,256]{2,0,1:T(8,128)(2,1)}) %all-gather.8.cloned.1.call-update) | async-done | bytes 33554448 | tf_op jit(solution)/shard_map/all_gather | solution.py:50
  686.6 209.1 %all-gather.6.cloned.1.call-done = bf16[64,256,1024]{2,0,1:T(8,128)(2,1)} async-done(((bf16[64,256,256]{2,0,1:T(8,128)(2,1)}), bf16[64,256,1024]{2,0,1:T(8,128)(2,1)}) %all-gather.6.cloned.1.call-update) | async-done | bytes 33554448 | tf_op jit(solution)/shard_map/all_gather | solution.py:54
  895.7 51.4 %fusion.5 = f32[64,256,256]{2,1,0:T(8,128)} fusion(bf16[64,1024,256]{2,0,1:T(8,128)(2,1)} %all-gather.8.cloned.1.call-done, bf16[64,256,1024]{2,0,1:T(8,128)(2,1)} %all-gather.6.cloned.1.call-done), kind=kOutput, calls=%fused_computation.7 | convolution fusion | flops 8589934592 | bytes 83886080 | tf_op jit(solution)/shard_map/hik,hkj->hij/dot_general | solution.py:28
  947.1 509.4 %all-gather.4.cloned.1.call-done = bf16[64,1024,256]{2,0,1:T(8,128)(2,1)} async-done(((bf16[64,256,256]{2,0,1:T(8,128)(2,1)}), bf16[64,1024,256]{2,0,1:T(8,128)(2,1)}) %all-gather.4.cloned.1.call-update) | async-done | bytes 33554448 | tf_op jit(solution)/shard_map/all_gather | solution.py:51
  1456.5 65.0 %multiply_convert_fusion.1 = bf16[64,256,256]{2,1,0:T(8,128)(2,1)} fusion(f32[64,256,256]{2,1,0:T(8,128)} %fusion.5, bf16[64,1024,256]{2,0,1:T(8,128)(2,1)} %all-gather.4.cloned.1.call-done, bf16[64,256,1024]{2,0,1:T(8,128)(2,1)} %constant_dynamic-slice_fusion), kind=kOutput, calls=%fused_computation.43 | convolution fusion | flops 8602517504 | bytes 92274688 | tf_op jit(solution)/shard_map/hik,hkj->hij/dot_general | solution.py:28
  1521.6 11.4 copy.45
  1533.0 7.4 all-to-all-start
  1540.4 0.7 dynamic_slice.20
  1541.2 0.1 multiply_multiply_fusion
  1541.3 11.5 fusion.37
  1552.7 78.6 %all-to-all-done = bf16[64,256,256]{2,0,1:T(8,128)(2,1)} async-done(((bf16[64,256,256]{2,0,1:T(8,128)(2,1)}), bf16[64,256,256]{2,0,1:T(8,128)(2,1)}, u32[]{:S(2)}, u32[]{:S(2)}) %all-to-all-start) | async-done | bytes 8388640 | tf_op jit(solution)/shard_map/all_to_all | solution.py:61
  1631.3 11.2 fusion.46
  1642.6 1.2 fusion.35
  1643.7 2.2 multiply_reduce_fusion.1
  1646.0 7.7 copy.47
  1653.8 5.6 fusion.30
  1659.4 14.5 multiply_reduce_fusion
  1673.9 12.7 copy.49
  1686.7 43.7 %psum.7 = f32[]{:T(128)} all-reduce(f32[]{:T(128)} %get-tuple-element.16), channel_id=1, replica_groups=mesh['gx'=4,'gy'=4,'gz'=2] {'gx','gy','gz'}, use_global_device_ids=true, to_apply=%region_5.6 | all-reduce | flops 1 | bytes 8 | tf_op jit(solution)/shard_map/psum | solution.py:82
  (37 shorter events, 0.2 us)
Async XLA Ops:
  7.2 54.5 %copy-start = (bf16[128,4,64]{0,2,1:T(8,128)(2,1)S(1)}, bf16[128,4,64]{0,2,1:T(8,128)(2,1)}, u32[]{:S(2)}) copy-start(bf16[128,4,64]{0,2,1:T(8,128)(2,1)} %param.10) | copy-start | bytes 196612
  7.2 679.4 %all-gather.8.cloned.1.call-start = ((), (), s32[]{:S(2)}) async-start(), calls=%async_computation.3 | async-start | bytes 41943040 | tf_op jit(solution)/shard_map/all_gather | solution.py:50
  7.2 12.6 copy-start.2
  8.1 30.8 %copy-start.7 = (f32[1024]{0:T(1024)}, f32[1024]{0:T(1024)S(1)}, u32[]{:S(2)}) copy-start(f32[1024]{0:T(1024)S(1)} %convert_element_type.61) | copy-start | bytes 12292
  8.1 31.6 %copy-start.8 = (f32[128]{0:T(128)S(1)}, f32[128]{0:T(128)}, u32[]{:S(2)}) copy-start(f32[128]{0:T(128)} %param.9) | copy-start | bytes 1540
  39.0 0.6 copy-start.5
  126.7 769.0 %all-gather.6.cloned.1.call-start = ((), (), s32[]{:S(2)}) async-start(), calls=%async_computation.2 | async-start | bytes 41943040 | tf_op jit(solution)/shard_map/all_gather | solution.py:54
  127.5 1329.1 %all-gather.4.cloned.1.call-start = ((), (), s32[]{:S(2)}) async-start(), calls=%async_computation.1 | async-start | bytes 41943040 | tf_op jit(solution)/shard_map/all_gather | solution.py:51
  128.2 93.1 %collective-permute-start = (bf16[64,256,256]{2,0,1:T(8,128)(2,1)}, bf16[64,256,256]{2,0,1:T(8,128)(2,1)S(1)}, u32[]{:S(2)}, u32[]{:S(2)}) collective-permute-start(bf16[64,256,256]{2,0,1:T(8,128)(2,1)} %get-tuple-element.11), channel_id=1, source_target_pairs={{0,2},{2,4},{4,6},{6,0},{1,3},{3,5},{5,7},{7,1},{8,10},{10,12},{12... | collective-permute-start | bytes 25165832 | tf_op jit(solution)/shard_map/ppermute | solution.py:14
  221.3 3.2 copy-start.3
  224.6 93.0 %collective-permute-start.1 = (bf16[64,256,256]{2,0,1:T(8,128)(2,1)S(1)}, bf16[64,256,256]{2,0,1:T(8,128)(2,1)}, u32[]{:S(2)}, u32[]{:S(2)}) collective-permute-start(bf16[64,256,256]{2,0,1:T(8,128)(2,1)S(1)} %collective-permute-done), channel_id=1, source_target_pairs={{0,2},{2,4},{4,6},{6,0},{1,3},{3,5},{5,7},{7,1},{8,10},{10,12},{12... | collective-permute-start | bytes 25165832 | tf_op jit(solution)/shard_map/ppermute | solution.py:14
  317.5 93.3 %collective-permute-start.2 = (bf16[64,256,256]{2,0,1:T(8,128)(2,1)}, bf16[64,256,256]{2,0,1:T(8,128)(2,1)}, u32[]{:S(2)}, u32[]{:S(2)}) collective-permute-start(bf16[64,256,256]{2,0,1:T(8,128)(2,1)} %collective-permute-done.1), channel_id=1, source_target_pairs={{0,2},{2,4},{4,6},{6,0},{1,3},{3,5},{5,7},{7,1},{8,10},{10,12},{12... | collective-permute-start | bytes 25165832 | tf_op jit(solution)/shard_map/ppermute | solution.py:14
  1521.6 19.6 %copy-start.6 = (f32[256]{0:T(256)S(1)}, f32[256]{0:T(256)}, u32[]{:S(2)}) copy-start(f32[256]{0:T(256)} %copy-done.5) | copy-start | bytes 3076
  1521.6 19.7 %copy-start.4 = (bf16[128,128]{1,0:T(8,128)(2,1)S(1)}, bf16[128,128]{1,0:T(8,128)(2,1)}, u32[]{:S(2)}) copy-start(bf16[128,128]{1,0:T(8,128)(2,1)} %param.11) | copy-start | bytes 98308
  1533.0 98.3 %all-to-all-start = ((bf16[64,256,256]{2,0,1:T(8,128)(2,1)}), bf16[64,256,256]{2,0,1:T(8,128)(2,1)}, u32[]{:S(2)}, u32[]{:S(2)}) async-start(bf16[64,256,256]{2,0,1:T(8,128)(2,1)} %copy.45), calls=%async_computation | async-start | bytes 16777216 | tf_op jit(solution)/shard_map/all_to_all | solution.py:61
  1646.0 7.8 copy-start.9
  1646.0 13.4 slice-start
  1646.0 13.4 slice-start.1
  1646.0 13.4 slice-start.2
  1653.8 5.6 slice-start.3
  1653.8 5.6 copy-start.10
  1659.4 71.5 %copy-start.1 = (bf16[128,4,64]{0,2,1:T(8,128)(2,1)S(1)}, bf16[128,4,64]{0,2,1:T(8,128)(2,1)}, u32[]{:S(2)}) copy-start(bf16[128,4,64]{0,2,1:T(8,128)(2,1)} %param.10) | copy-start | bytes 196612
Sparse Core Ops, SparseCore 0:
  126.8 559.7 all-gather.7
  688.7 206.9 all-gather.5
  897.9 558.6 all-gather.3
